TPU v7x, 32 devices: a whole 2x2x4 slice. The times are simulated.
32 devices in a mesh: grp: 2 (over y), sp: 16 (over z, x, core).
Axes of the slice: x: 2, y: 2, z: 4, core: 2. Of those that a mesh axis runs over, the one named last changes fastest.
Arguments:
- alpha: float32 [20, 16, 4096], P('grp', None, 'sp'), may hold values from -6 to 6
- ensemble: bfloat16 [20, 3, 16, 4096], P('grp', None, None, 'sp'), may hold values from -6 to 6
- static_std: float32 [3, 16, 4096], P(None, 'grp', 'sp'), may hold values from 0.2 to 1
- control: float32 [3, 16, 4096], P(None, 'grp', 'sp'), may hold values from -6 to 6
- loc_spectrum: float32 [1024], replicated, may hold values from 0.00024414062 to 0.001953125
- obs_cell: int32 [32768], P(('grp', 'sp')), may hold values from 0 to 65535, as said below
- obs_step: int32 [32768], P(('grp', 'sp')), may hold values from 0 to 2
- innovation: float32 [32768], P(('grp', 'sp')), may hold values from -6 to 6
- obs_weight: float32 [32768], P(('grp', 'sp')), may hold values from 0.5 to 4
Outputs:
- grad_alpha: float32 [20, 16, 4096], P('grp', None, 'sp')
- grad_control: float32 [3, 16, 4096], P(None, 'grp', 'sp')
Inputs may be any that keep to these rules, and one draw needn't show every extreme that they name: `obs_cell`: an entry is row * 4096 + column. Entries 1024 * b to 1024 * (b + 1) - 1 lie in the tile of 8 rows from row 8 * (b // 16) and 256 columns from column 256 * (b % 16).
All inputs are finite; a program needn't handle non-finite values.
Results may differ from a plain program's by a relative error of at most 0.0075.
Values may be sent and summed in bfloat16 or wider, within the bound.
A program may use at most 128 MiB of HBM per device.

v0:
```python
import math
import jax
import jax.numpy as jnp
from jax import lax
from jax.sharding import PartitionSpec as P

NX = 4096
courant = 0.4


def extended(block, sides, width):
    for axis, dim in sides:
        count = lax.axis_size(axis)
        forward = [(i, i + 1) for i in range(count - 1)]
        forward.append((count - 1, 0))
        backward = [(target, source) for source, target in forward]
        low = lax.ppermute(
            lax.slice_in_dim(block, block.shape[dim] - width, None, axis=dim), axis, forward
        )
        high = lax.ppermute(lax.slice_in_dim(block, 0, width, axis=dim), axis, backward)
        block = jnp.concatenate([low, block, high], axis=dim)
    return block


def spectral_filter(rows_data, loc_spectrum):
    length_x = rows_data.shape[1]
    kept_waves = loc_spectrum.shape[0]
    freq_block = math.gcd(kept_waves, 256)
    positions = jnp.arange(length_x, dtype=jnp.int32)
    filtered = jnp.zeros(rows_data.shape, jnp.float32)
    for start_wave in range(0, kept_waves, freq_block):
        waves = start_wave + jnp.arange(freq_block, dtype=jnp.int32)
        phases = positions[:, None] * waves[None, :] % length_x
        radians = 2.0 * math.pi / length_x * phases.astype(jnp.float32)
        fourier_basis = jnp.concatenate([jnp.cos(radians), jnp.sin(radians)], axis=1)
        weights = loc_spectrum[start_wave : start_wave + freq_block]
        weights = jnp.concatenate([weights, weights])
        coeffs = jnp.dot(
            rows_data,
            fourier_basis,
            precision=lax.Precision.HIGHEST,
            preferred_element_type=jnp.float32,
        )
        filtered = filtered + jnp.dot(
            coeffs * weights[None, :],
            fourier_basis.T,
            precision=lax.Precision.HIGHEST,
            preferred_element_type=jnp.float32,
        )
    return filtered


def inner(field):
    return field[..., 1:-1, 1:-1]


def diff_x(field):
    return 0.5 * (field[..., 1:-1, 2:] - field[..., 1:-1, :-2])


def diff_y(field):
    return 0.5 * (field[..., 2:, 1:-1] - field[..., :-2, 1:-1])


def clip_rows(stack, margin, first_row, total_rows):
    rows_index = first_row - margin + jnp.arange(stack.shape[1], dtype=jnp.int32)
    valid = jnp.logical_and(rows_index >= 0, rows_index < total_rows).astype(jnp.float32)
    return stack * valid[None, :, None]


def coriolis_rows(first_row, margin, count, total_rows):
    rows_index = first_row - margin + jnp.arange(count, dtype=jnp.int32)
    return (0.1 + 0.2 * (rows_index.astype(jnp.float32) + 0.5) / total_rows)[:, None]


def forward_a(stack, margin, first_row, total_rows):
    height, eastward, northward = (stack[0], stack[1], stack[2])
    new_height = inner(height) - courant * (diff_x(eastward) + diff_y(northward))
    result = jnp.stack([new_height, inner(eastward), inner(northward)])
    return clip_rows(result, margin - 1, first_row, total_rows)


def forward_b(stack, margin, first_row, total_rows):
    height, eastward, northward = (stack[0], stack[1], stack[2])
    rotation = coriolis_rows(first_row, margin - 1, stack.shape[1] - 2, total_rows)
    new_east = inner(eastward) - courant * diff_x(height) + rotation * inner(northward)
    new_north = inner(northward) - courant * diff_y(height) - rotation * inner(eastward)
    result = jnp.stack([inner(height), new_east, new_north])
    return clip_rows(result, margin - 1, first_row, total_rows)


def backward_a(stack, margin, first_row, total_rows):
    back_h, back_u, back_w = (stack[0], stack[1], stack[2])
    adj_height = inner(back_h) + courant * (diff_x(back_u) + diff_y(back_w))
    result = jnp.stack([adj_height, inner(back_u), inner(back_w)])
    return clip_rows(result, margin - 1, first_row, total_rows)


def backward_b(stack, margin, first_row, total_rows):
    adj_height, back_u, back_w = (stack[0], stack[1], stack[2])
    rotation = coriolis_rows(first_row, margin - 1, stack.shape[1] - 2, total_rows)
    adj_east = inner(back_u) - rotation * inner(back_w) + courant * diff_x(adj_height)
    adj_north = inner(back_w) + rotation * inner(back_u) + courant * diff_y(adj_height)
    result = jnp.stack([inner(adj_height), adj_east, adj_north])
    return clip_rows(result, margin - 1, first_row, total_rows)


def deep_rim(stack):
    return extended(stack, (("grp", 1), ("sp", 2)), 4)


def per_device(
    alpha, ensemble, static_std, control, loc_spectrum, obs_cell, obs_step, innovation, obs_weight
):
    members_local = alpha.shape[0]
    groups = lax.axis_size("grp")
    spread = 1.0 / math.sqrt(members_local * groups - 1)
    tile_rows, tile_cols = (control.shape[1], control.shape[2])
    total_rows = tile_rows * groups
    first_row = lax.axis_index("grp") * tile_rows
    first_col = lax.axis_index("sp") * tile_cols

    def localize_items(items):
        dims = items.shape
        flat = items.reshape(dims[0] * dims[1], dims[2])
        return spectral_filter(flat, loc_spectrum).reshape(dims)

    def to_rows(columns):
        return localize_items(
            lax.all_to_all(columns, "sp", split_axis=1, concat_axis=2, tiled=True)
        )

    localized = lax.all_to_all(
        to_rows(alpha).astype(jnp.bfloat16), "sp", split_axis=2, concat_axis=1, tiled=True
    )
    partial_value = jnp.einsum(
        "mvyx,myx->vyx", ensemble, localized, preferred_element_type=jnp.float32
    )
    summed = lax.psum_scatter(partial_value, "grp", scatter_dimension=1, tiled=True)
    increment = static_std * control + spread * summed
    padded = clip_rows(deep_rim(increment), 4, first_row, total_rows)
    middle = forward_b(forward_a(padded, 4, first_row, total_rows), 3, first_row, total_rows)
    first_state = middle[:, 2:-2, 2:-2]
    second_state = forward_b(forward_a(middle, 2, first_row, total_rows), 1, first_row, total_rows)
    states = (increment, first_state, second_state)
    local_index = (obs_cell // NX - first_row) * tile_cols + (obs_cell % NX - first_col)
    observed = jnp.zeros(innovation.shape, jnp.float32)
    for moment in range(3):
        values = states[moment][0].reshape(-1)[local_index]
        observed = jnp.where(obs_step == moment, values, observed)
    misfit = obs_weight * (observed - innovation)
    forcings = []
    for moment in range(3):
        spread_obs = jnp.where(obs_step == moment, misfit, jnp.zeros_like(misfit))
        height_force = (
            jnp.zeros((tile_rows * tile_cols,), jnp.float32).at[local_index].add(spread_obs)
        )
        forcings.append(height_force.reshape(tile_rows, tile_cols))
    zero_field = jnp.zeros((tile_rows, tile_cols), jnp.float32)
    last_adjoint = jnp.stack([forcings[2], zero_field, zero_field])
    padded = clip_rows(
        deep_rim(jnp.concatenate([last_adjoint, forcings[1][None]], axis=0)),
        4,
        first_row,
        total_rows,
    )
    middle = backward_b(backward_a(padded[:3], 4, first_row, total_rows), 3, first_row, total_rows)
    middle = middle.at[0].add(padded[3, 2:-2, 2:-2])
    adjoint = backward_b(backward_a(middle, 2, first_row, total_rows), 1, first_row, total_rows)
    adjoint = adjoint.at[0].add(forcings[0])
    grad_control = control + static_std * adjoint
    half = adjoint.astype(jnp.bfloat16)
    weighted = jnp.einsum(
        "mvyx,vyx->myx",
        ensemble,
        lax.all_gather(half, "grp", axis=1, tiled=True),
        preferred_element_type=jnp.float32,
    )
    filtered = lax.all_to_all(to_rows(weighted), "sp", split_axis=2, concat_axis=1, tiled=True)
    grad_alpha = alpha + spread * filtered
    return (grad_alpha, grad_control)


def solution(mesh):
    placed = (
        P("grp", None, "sp"),
        P("grp", None, None, "sp"),
        P(None, "grp", "sp"),
        P(None, "grp", "sp"),
        P(),
        P(("grp", "sp")),
        P(("grp", "sp")),
        P(("grp", "sp")),
        P(("grp", "sp")),
    )
    return jax.shard_map(
        per_device,
        mesh=mesh,
        in_specs=placed,
        out_specs=(P("grp", None, "sp"), P(None, "grp", "sp")),
        check_vma=False,
    )
```

profile of v0, /device:TPU:0, one launch (start us, length us, event | category | flops | bytes accessed | tf_op | source)
XLA Modules:
  0.0 365.8 jit_solution(6767588958854362796)
XLA Ops:
  8.9 7.4 %all-to-all-start = ((f32[10,16,256]{2,0,1:T(8,128)}), f32[10,16,256]{2,0,1:T(8,128)S(1)}, u32[]{:S(2)}, u32[]{:S(2)}) async-start(f32[10,16,256]{2,0,1:T(8,128)} %copy.22), calls=%async_computation | async-start | bytes 524288 | tf_op jit(solution)/shard_map/all_to_all | solution.py:130
  16.3 17.6 %fusion.37 = (f32[4096,256]{1,0:T(8,128)}, f32[4096,256]{1,0:T(8,128)}) fusion(), kind=kLoop, calls=%fused_computation.65 | loop fusion | flops 14680064 | bytes 8388608 | tf_op jit(solution)/shard_map/sin | solution.py:35
  34.0 17.9 %fusion.44 = (f32[4096,256]{1,0:T(8,128)}, f32[4096,256]{1,0:T(8,128)}) fusion(s32[256]{0:T(256)S(1)} %iota_add_fusion.2), kind=kLoop, calls=%fused_computation.72 | loop fusion | flops 14680064 | bytes 8389632 | tf_op jit(solution)/shard_map/cos | solution.py:35
  51.8 17.9 %fusion.42 = (f32[4096,256]{1,0:T(8,128)}, f32[4096,256]{1,0:T(8,128)}) fusion(s32[256]{0:T(256)S(1)} %iota_add_fusion.1), kind=kLoop, calls=%fused_computation.70 | loop fusion | flops 14680064 | bytes 8389632 | tf_op jit(solution)/shard_map/cos | solution.py:35
  69.7 17.9 %fusion.40 = (f32[4096,256]{1,0:T(8,128)}, f32[4096,256]{1,0:T(8,128)}) fusion(s32[256]{0:T(256)S(1)} %iota_add_fusion), kind=kLoop, calls=%fused_computation.68 | loop fusion | flops 14680064 | bytes 8389632 | tf_op jit(solution)/shard_map/cos | solution.py:35
  88.0 7.5 %fusion.45 = f32[512,10]{0,1:T(8,128)S(1)} fusion(f32[10,4096]{1,0:T(8,128)S(1)} %bitcast.175, f32[4096,256]{1,0:T(8,128)} %get-tuple-element.106, f32[4096,256]{1,0:T(8,128)} %get-tuple-element.107, f32[512]{0:T(512)S(1)} %get-tuple-element.102), kind=kOutput, calls=%fused_computation.73 | convolution fusion | flops 253760512 | bytes 8574976 | tf_op jit(solution)/shard_map/dot_general | solution.py:38
  95.5 7.0 %fusion.35 = f32[10,4096]{1,0:T(8,128)S(1)} fusion(f32[512,10]{0,1:T(8,128)S(1)} %fusion.45, f32[4096,256]{1,0:T(8,128)S(1)} %copy-done, f32[4096,256]{1,0:T(8,128)S(1)} %copy-done.2), kind=kOutput, calls=%fused_computation.63 | convolution fusion | flops 253755392 | bytes 8572928 | tf_op jit(solution)/shard_map/dot_general | solution.py:44
  102.5 4.5 %fusion.47 = f32[512,10]{0,1:T(8,128)S(1)} fusion(f32[10,4096]{1,0:T(8,128)S(1)} %bitcast.176, f32[4096,256]{1,0:T(8,128)S(1)} %copy-done.14, f32[4096,256]{1,0:T(8,128)S(1)} %copy-done.12, f32[512]{0:T(512)S(1)} %get-tuple-element.103), kind=kOutput, calls=%fused_computation.75 | convolution fusion | flops 253760512 | bytes 8574976 | tf_op jit(solution)/shard_map/dot_general | solution.py:38
  107.0 7.2 %convolution_add_fusion.5 = f32[10,4096]{1,0:T(8,128)S(1)} fusion(f32[10,4096]{1,0:T(8,128)S(1)} %fusion.35, f32[512,10]{0,1:T(8,128)S(1)} %fusion.47, f32[4096,256]{1,0:T(8,128)S(1)} %copy-done.14, f32[4096,256]{1,0:T(8,128)S(1)} %copy-done.12), kind=kOutput, calls=%fused_computation.28 | convolution fusion | flops 253796352 | bytes 8736768 | tf_op jit(solution)/shard_map/dot_general | solution.py:44
  114.2 4.5 %fusion.49 = f32[512,10]{0,1:T(8,128)S(1)} fusion(f32[10,4096]{1,0:T(8,128)S(1)} %bitcast.177, f32[4096,256]{1,0:T(8,128)S(1)} %copy-done.10, f32[4096,256]{1,0:T(8,128)S(1)} %copy-done.8, f32[512]{0:T(512)S(1)} %get-tuple-element.104), kind=kOutput, calls=%fused_computation.77 | convolution fusion | flops 253760512 | bytes 8574976 | tf_op jit(solution)/shard_map/dot_general | solution.py:38
  118.7 7.4 %convolution_add_fusion.4 = f32[10,4096]{1,0:T(8,128)S(1)} fusion(f32[10,4096]{1,0:T(8,128)S(1)} %convolution_add_fusion.5, f32[512,10]{0,1:T(8,128)S(1)} %fusion.49, f32[4096,256]{1,0:T(8,128)S(1)} %copy-done.10, f32[4096,256]{1,0:T(8,128)S(1)} %copy-done.8), kind=kOutput, calls=%fused_computation.27 | convolution fusion | flops 253796352 | bytes 8736768 | tf_op jit(solution)/shard_map/dot_general | solution.py:44
  126.2 4.5 %fusion.51 = f32[512,10]{0,1:T(8,128)S(1)} fusion(f32[10,4096]{1,0:T(8,128)S(1)} %bitcast.178, f32[4096,256]{1,0:T(8,128)S(1)} %copy-done.6, f32[4096,256]{1,0:T(8,128)S(1)} %copy-done.4, f32[512]{0:T(512)S(1)} %get-tuple-element.105), kind=kOutput, calls=%fused_computation.79 | convolution fusion | flops 253760512 | bytes 8574976 | tf_op jit(solution)/shard_map/dot_general | solution.py:38
  130.7 7.2 %fusion.2 = bf16[10,1,4096]{2,0,1:T(8,128)(2,1)S(1)} fusion(f32[10,4096]{1,0:T(8,128)S(1)} %convolution_add_fusion.4, f32[512,10]{0,1:T(8,128)S(1)} %fusion.51, f32[4096,256]{1,0:T(8,128)S(1)} %copy-done.6, f32[4096,256]{1,0:T(8,128)S(1)} %copy-done.4), kind=kOutput, calls=%fused_computation.30 | convolution fusion | flops 253837312 | bytes 8654848 | tf_op jit(solution)/shard_map/dot_general | solution.py:44
  137.8 2.8 copy.24
  141.2 22.5 %reduce.10 = bf16[4096,10]{1,0:T(8,128)(2,1)S(1)} reduce(bf16[4096,1,10]{2,1,0:T(2,128)(2,1)S(1)} %bitcast.160, bf16[]{:T(256)} %broadcast.393), dimensions={1}, to_apply=%bitcast.136.reduce_sub_computation | reduce | bytes 163842
  163.6 2.5 reshape.233
  166.1 6.0 %all-to-all-start.1 = ((bf16[16,2,1280]{2,1,0:T(2,128)(2,1)}), bf16[16,2,1280]{2,1,0:T(2,128)(2,1)S(1)}, u32[]{:S(2)}, u32[]{:S(2)}) async-start(bf16[16,2,1280]{2,1,0:T(2,128)(2,1)} %reshape.233), calls=%async_computation.1 | async-start | bytes 163840 | tf_op jit(solution)/shard_map/all_to_all | solution.py:133
  172.2 7.0 %all-to-all-done.1 = bf16[16,2,1280]{2,1,0:T(2,128)(2,1)S(1)} async-done(((bf16[16,2,1280]{2,1,0:T(2,128)(2,1)}), bf16[16,2,1280]{2,1,0:T(2,128)(2,1)S(1)}, u32[]{:S(2)}, u32[]{:S(2)}) %all-to-all-start.1) | async-done | bytes 81952 | tf_op jit(solution)/shard_map/all_to_all | solution.py:133
  179.2 2.2 reshape.234
  181.4 2.1 copy.25
  184.4 7.6 %reduce-scatter.2.cloned.1.call-done = f32[3,8,256]{2,1,0:T(8,128)} async-done(((f32[3,16,256]{2,1,0:T(8,128)}), f32[3,8,256]{2,1,0:T(8,128)}) %reduce-scatter.2.cloned.1.call-update) | async-done | bytes 24592 | tf_op jit(solution)/shard_map/reduce_scatter | solution.py:139
  193.0 1.8 collective-permute-start.1
  196.8 4.4 %collective-permute-start.3 = (f32[3,16,4]{2,1,0:T(8,128)S(1)}, f32[3,16,4]{2,1,0:T(8,128)S(1)}, u32[]{:S(2)}, u32[]{:S(2)}) collective-permute-start(f32[3,16,4]{2,1,0:T(8,128)S(1)} %get-tuple-element.67), channel_id=1, source_target_pairs={{1,0},{2,1},{3,2},{4,3},{5,4},{6,5},{7,6},{8,7},{9,8},{10,9},{11,1... | collective-permute-start | bytes 2312 | tf_op jit(solution)/shard_map/ppermute | solution.py:20
  201.2 6.1 %gather_fusion.2 = f32[1024]{0:T(1024)S(1)} fusion(f32[2048]{0:T(1024)S(1)} %bitcast.158, s32[1024]{0:T(1024)S(1)} %get-tuple-element.30), kind=kCustom, calls=%fused_computation.2 | custom fusion | bytes 12288 | tf_op jit(solution)/shard_map/gather | solution.py:149
  208.4 6.2 %gather_fusion = f32[1024]{0:T(1024)S(1)} fusion(f32[2048]{0:T(1024)S(1)} %bitcast.159, s32[1024]{0:T(1024)S(1)} %get-tuple-element.30), kind=kCustom, calls=%fused_computation | custom fusion | bytes 12288 | tf_op jit(solution)/shard_map/gather | solution.py:149
  214.6 6.2 %gather_fusion.1 = f32[1024]{0:T(1024)S(1)} fusion(f32[2048]{0:T(1024)S(1)} %bitcast.157, s32[1024]{0:T(1024)S(1)} %get-tuple-element.30), kind=kCustom, calls=%fused_computation.1 | custom fusion | bytes 12288 | tf_op jit(solution)/shard_map/gather | solution.py:149
  220.8 6.0 %scatter_custom_fusion = f32[2048]{0:T(1024)S(1)} fusion(s32[1024]{0:T(1024)S(1)} %get-tuple-element.31, f32[1024]{0:T(1024)S(1)} %get-tuple-element.90, f32[]{:T(128)} %constant.175.clone.1), kind=kCustom, calls=%fused_computation.226 | custom fusion | flops 1024 | bytes 8196 | tf_op jit(solution)/shard_map/scatter-add | solution.py:156
  226.8 6.0 %scatter_custom_fusion.1 = f32[2048]{0:T(1024)S(1)} fusion(s32[1024]{0:T(1024)S(1)} %get-tuple-element.31, f32[1024]{0:T(1024)S(1)} %get-tuple-element.91, f32[]{:T(128)} %constant.175.clone.1), kind=kCustom, calls=%fused_computation.224 | custom fusion | flops 1024 | bytes 8196 | tf_op jit(solution)/shard_map/scatter-add | solution.py:156
  232.8 2.0 collective-permute-start.4
  236.6 1.9 collective-permute-done.5
  238.6 4.4 %collective-permute-start.7 = (f32[4,16,4]{2,1,0:T(8,128)S(1)}, f32[4,16,4]{2,1,0:T(8,128)S(1)}, u32[]{:S(2)}, u32[]{:S(2)}) collective-permute-start(f32[4,16,4]{2,1,0:T(8,128)S(1)} %get-tuple-element.65), channel_id=1, source_target_pairs={{1,0},{2,1},{3,2},{4,3},{5,4},{6,5},{7,6},{8,7},{9,8},{10,9},{11,1... | collective-permute-start | bytes 3080 | tf_op jit(solution)/shard_map/ppermute | solution.py:20
  243.0 6.0 %scatter_custom_fusion.2 = f32[2048]{0:T(1024)S(1)} fusion(s32[1024]{0:T(1024)S(1)} %get-tuple-element.31, f32[1024]{0:T(1024)S(1)} %get-tuple-element.26, f32[]{:T(128)} %constant.175.clone.1), kind=kCustom, calls=%fused_computation.222 | custom fusion | flops 1024 | bytes 8196 | tf_op jit(solution)/shard_map/scatter-add | solution.py:156
  250.6 4.4 %all_gather.3 = bf16[3,16,256]{2,1,0:T(8,128)(2,1)S(1)} all-gather(bf16[3,8,256]{2,1,0:T(8,128)(2,1)S(1)} %get-tuple-element.71), channel_id=1, replica_groups=mesh['grp'=2,'sp'=16] {'grp'}, dimensions={1}, use_global_device_ids=true | all-gather | bytes 36864 | tf_op jit(solution)/shard_map/all_gather | solution.py:176
  255.2 12.6 %all_to_all.19 = f32[10,16,256]{2,0,1:T(8,128)S(1)} all-to-all(f32[10,16,256]{2,0,1:T(8,128)S(1)} %bitcast.170), channel_id=1, replica_groups=mesh['grp'=2,'sp'=16] {'sp'}, dimensions={1} | all-to-all | bytes 327680 | tf_op jit(solution)/shard_map/all_to_all | solution.py:130
  268.1 4.9 %fusion.52 = f32[10,512]{1,0:T(8,128)S(1)} fusion(f32[10,4096]{1,0:T(8,128)S(1)} %bitcast.164, f32[4096,256]{1,0:T(8,128)} %get-tuple-element.97, f32[4096,256]{1,0:T(8,128)S(1)} %copy-done.5, f32[512]{0:T(512)S(1)} %get-tuple-element.105), kind=kOutput, calls=%fused_computation.80 | convolution fusion | flops 253760512 | bytes 8574976 | tf_op jit(solution)/shard_map/dot_general | solution.py:38
  273.1 4.1 %fusion.50 = f32[10,512]{1,0:T(8,128)S(1)} fusion(f32[10,4096]{1,0:T(8,128)S(1)} %bitcast.165, f32[4096,256]{1,0:T(8,128)S(1)} %copy-done.11, f32[4096,256]{1,0:T(8,128)S(1)} %copy-done.9, f32[512]{0:T(512)S(1)} %get-tuple-element.104), kind=kOutput, calls=%fused_computation.78 | convolution fusion | flops 253760512 | bytes 8574976 | tf_op jit(solution)/shard_map/dot_general | solution.py:38
  277.2 4.1 %fusion.48 = f32[10,512]{1,0:T(8,128)S(1)} fusion(f32[10,4096]{1,0:T(8,128)S(1)} %bitcast.166, f32[4096,256]{1,0:T(8,128)S(1)} %copy-done.15, f32[4096,256]{1,0:T(8,128)S(1)} %copy-done.13, f32[512]{0:T(512)S(1)} %get-tuple-element.103), kind=kOutput, calls=%fused_computation.76 | convolution fusion | flops 253760512 | bytes 8574976 | tf_op jit(solution)/shard_map/dot_general | solution.py:38
  281.3 4.3 %fusion.46 = f32[10,512]{1,0:T(8,128)S(1)} fusion(f32[10,4096]{1,0:T(8,128)S(1)} %bitcast.167, f32[4096,256]{1,0:T(8,128)S(1)} %copy-done.1, f32[4096,256]{1,0:T(8,128)S(1)} %copy-done.3, f32[512]{0:T(512)S(1)} %get-tuple-element.102), kind=kOutput, calls=%fused_computation.74 | convolution fusion | flops 253760512 | bytes 8574976 | tf_op jit(solution)/shard_map/dot_general | solution.py:38
  285.5 7.0 %fusion.33 = f32[10,4096]{1,0:T(8,128)S(1)} fusion(f32[10,512]{1,0:T(8,128)S(1)} %fusion.46, f32[4096,256]{1,0:T(8,128)S(1)} %copy-done.1, f32[4096,256]{1,0:T(8,128)S(1)} %copy-done.3), kind=kOutput, calls=%fused_computation.61 | convolution fusion | flops 253755392 | bytes 8572928 | tf_op jit(solution)/shard_map/dot_general | solution.py:44
  292.5 7.2 %convolution_add_fusion.2 = f32[10,4096]{1,0:T(8,128)S(1)} fusion(f32[10,4096]{1,0:T(8,128)S(1)} %fusion.33, f32[10,512]{1,0:T(8,128)S(1)} %fusion.48, f32[4096,256]{1,0:T(8,128)S(1)} %copy-done.15, f32[4096,256]{1,0:T(8,128)S(1)} %copy-done.13), kind=kOutput, calls=%fused_computation.25 | convolution fusion | flops 253796352 | bytes 8736768 | tf_op jit(solution)/shard_map/dot_general | solution.py:44
  299.7 7.0 %convolution_add_fusion.1 = f32[10,4096]{1,0:T(8,128)S(1)} fusion(f32[10,4096]{1,0:T(8,128)S(1)} %convolution_add_fusion.2, f32[10,512]{1,0:T(8,128)S(1)} %fusion.50, f32[4096,256]{1,0:T(8,128)S(1)} %copy-done.11, f32[4096,256]{1,0:T(8,128)S(1)} %copy-done.9), kind=kOutput, calls=%fused_computation.24 | convolution fusion | flops 253796352 | bytes 8736768 | tf_op jit(solution)/shard_map/dot_general | solution.py:44
  306.7 7.0 %fusion = f32[10,1,4096]{2,0,1:T(8,128)S(1)} fusion(f32[10,4096]{1,0:T(8,128)S(1)} %convolution_add_fusion.1, f32[10,512]{1,0:T(8,128)S(1)} %fusion.52, f32[4096,256]{1,0:T(8,128)S(1)} %copy-done.7, f32[4096,256]{1,0:T(8,128)S(1)} %copy-done.5), kind=kOutput, calls=%fused_computation.23 | convolution fusion | flops 253796352 | bytes 8736768 | tf_op jit(solution)/shard_map/dot_general | solution.py:44
  313.7 2.5 copy.27
  316.7 19.6 %reduce.11 = f32[4096,10]{1,0:T(8,128)} reduce(f32[4096,1,10]{2,1,0:T(1,128)S(1)} %bitcast.161, f32[]{:T(128)} %broadcast.394), dimensions={1}, to_apply=%bitcast.138.reduce_sub_computation | reduce | bytes 327684
  336.4 3.4 reshape.235
  339.8 11.1 %all_to_all.40 = f32[16,1,2560]{2,1,0:T(1,128)S(1)} all-to-all(f32[16,1,2560]{2,1,0:T(1,128)S(1)} %reshape.235), channel_id=1, replica_groups=mesh['grp'=2,'sp'=16] {'sp'}, dimensions={0} | all-to-all | bytes 327680 | tf_op jit(solution)/shard_map/all_to_all | solution.py:179
  352.0 3.3 reshape.236
  355.2 2.0 copy.28
  (144 shorter events, 14.2 us)
Async XLA Ops:
  8.9 78.7 %all-to-all-start = ((f32[10,16,256]{2,0,1:T(8,128)}), f32[10,16,256]{2,0,1:T(8,128)S(1)}, u32[]{:S(2)}, u32[]{:S(2)}) async-start(f32[10,16,256]{2,0,1:T(8,128)} %copy.22), calls=%async_computation | async-start | bytes 524288 | tf_op jit(solution)/shard_map/all_to_all | solution.py:130
  16.3 17.7 %copy-start.23 = (f32[1024]{0:T(1024)S(1)}, f32[1024]{0:T(1024)}, u32[]{:S(2)}) copy-start(f32[1024]{0:T(1024)} %param.17) | copy-start | bytes 12292
  69.7 17.9 %copy-start.24 = (s32[1024]{0:T(1024)S(1)}, s32[1024]{0:T(1024)}, u32[]{:S(2)}) copy-start(s32[1024]{0:T(1024)} %param.18) | copy-start | bytes 12292
  87.9 7.5 %copy-start = (f32[4096,256]{1,0:T(8,128)S(1)}, f32[4096,256]{1,0:T(8,128)}, u32[]{:S(2)}) copy-start(f32[4096,256]{1,0:T(8,128)} %get-tuple-element.106) | copy-start | bytes 12582916
  87.9 7.5 %copy-start.2 = (f32[4096,256]{1,0:T(8,128)S(1)}, f32[4096,256]{1,0:T(8,128)}, u32[]{:S(2)}) copy-start(f32[4096,256]{1,0:T(8,128)} %get-tuple-element.107) | copy-start | bytes 12582916
  95.5 7.0 %copy-start.12 = (f32[4096,256]{1,0:T(8,128)S(1)}, f32[4096,256]{1,0:T(8,128)}, u32[]{:S(2)}) copy-start(f32[4096,256]{1,0:T(8,128)} %get-tuple-element.100) | copy-start | bytes 12582916
  95.5 7.0 %copy-start.14 = (f32[4096,256]{1,0:T(8,128)S(1)}, f32[4096,256]{1,0:T(8,128)}, u32[]{:S(2)}) copy-start(f32[4096,256]{1,0:T(8,128)} %get-tuple-element.101) | copy-start | bytes 12582916
  107.0 7.2 %copy-start.8 = (f32[4096,256]{1,0:T(8,128)S(1)}, f32[4096,256]{1,0:T(8,128)}, u32[]{:S(2)}) copy-start(f32[4096,256]{1,0:T(8,128)} %get-tuple-element.98) | copy-start | bytes 12582916
  107.0 7.2 %copy-start.10 = (f32[4096,256]{1,0:T(8,128)S(1)}, f32[4096,256]{1,0:T(8,128)}, u32[]{:S(2)}) copy-start(f32[4096,256]{1,0:T(8,128)} %get-tuple-element.99) | copy-start | bytes 12582916
  118.7 7.4 %copy-start.4 = (f32[4096,256]{1,0:T(8,128)S(1)}, f32[4096,256]{1,0:T(8,128)}, u32[]{:S(2)}) copy-start(f32[4096,256]{1,0:T(8,128)} %get-tuple-element.96) | copy-start | bytes 12582916
  118.7 7.4 %copy-start.6 = (f32[4096,256]{1,0:T(8,128)S(1)}, f32[4096,256]{1,0:T(8,128)}, u32[]{:S(2)}) copy-start(f32[4096,256]{1,0:T(8,128)} %get-tuple-element.97) | copy-start | bytes 12582916
  141.2 42.5 %copy-start.16 = (bf16[10,3,16,256]{3,2,1,0:T(8,128)(2,1)S(1)}, bf16[10,3,16,256]{3,2,1,0:T(8,128)(2,1)}, u32[]{:S(2)}) copy-start(bf16[10,3,16,256]{3,2,1,0:T(8,128)(2,1)} %param.14) | copy-start | bytes 737284
  141.2 50.8 %copy-start.18 = (f32[3,8,256]{2,1,0:T(8,128)S(1)}, f32[3,8,256]{2,1,0:T(8,128)}, u32[]{:S(2)}) copy-start(f32[3,8,256]{2,1,0:T(8,128)} %param.16) | copy-start | bytes 73732
  141.2 50.8 %copy-start.19 = (f32[3,8,256]{2,1,0:T(8,128)S(1)}, f32[3,8,256]{2,1,0:T(8,128)}, u32[]{:S(2)}) copy-start(f32[3,8,256]{2,1,0:T(8,128)} %param.15) | copy-start | bytes 73732
  166.1 13.1 %all-to-all-start.1 = ((bf16[16,2,1280]{2,1,0:T(2,128)(2,1)}), bf16[16,2,1280]{2,1,0:T(2,128)(2,1)S(1)}, u32[]{:S(2)}, u32[]{:S(2)}) async-start(bf16[16,2,1280]{2,1,0:T(2,128)(2,1)} %reshape.233), calls=%async_computation.1 | async-start | bytes 163840 | tf_op jit(solution)/shard_map/all_to_all | solution.py:133
  172.1 19.9 %reduce-scatter.2.cloned.1.call-start = ((), (), s32[]{:S(2)}) async-start(), calls=%async_computation.5 | async-start | bytes 73728 | tf_op jit(solution)/shard_map/reduce_scatter | solution.py:139
  192.7 3.8 %collective-permute-start = (f32[3,4,256]{2,1,0:T(4,128)S(1)}, f32[3,4,256]{2,1,0:T(4,128)S(1)}, u32[]{:S(2)}, u32[]{:S(2)}) collective-permute-start(f32[3,4,256]{2,1,0:T(4,128)S(1)} %get-tuple-element.88), channel_id=1, source_target_pairs={{0,16},{16,0},{1,17},{17,1},{2,18},{18,2},{3,19},{19,3},{4,20},{20... | collective-permute-start | bytes 36872 | tf_op jit(solution)/shard_map/ppermute | solution.py:17
  193.0 3.7 %collective-permute-start.1 = (f32[3,4,256]{2,1,0:T(4,128)S(1)}, f32[3,4,256]{2,1,0:T(4,128)S(1)}, u32[]{:S(2)}, u32[]{:S(2)}) collective-permute-start(f32[3,4,256]{2,1,0:T(4,128)S(1)} %get-tuple-element.89), channel_id=1, source_target_pairs={{16,0},{0,16},{17,1},{1,17},{18,2},{2,18},{19,3},{3,19},{20,4},{4,... | collective-permute-start | bytes 36872 | tf_op jit(solution)/shard_map/ppermute | solution.py:20
  196.7 10.6 %collective-permute-start.2 = (f32[3,16,4]{2,1,0:T(8,128)S(1)}, f32[3,16,4]{2,1,0:T(8,128)S(1)}, u32[]{:S(2)}, u32[]{:S(2)}) collective-permute-start(f32[3,16,4]{2,1,0:T(8,128)S(1)} %get-tuple-element.66), channel_id=1, source_target_pairs={{0,1},{1,2},{2,3},{3,4},{4,5},{5,6},{6,7},{7,8},{8,9},{9,10},{10,1... | collective-permute-start | bytes 2312 | tf_op jit(solution)/shard_map/ppermute | solution.py:17
  196.8 10.6 %collective-permute-start.3 = (f32[3,16,4]{2,1,0:T(8,128)S(1)}, f32[3,16,4]{2,1,0:T(8,128)S(1)}, u32[]{:S(2)}, u32[]{:S(2)}) collective-permute-start(f32[3,16,4]{2,1,0:T(8,128)S(1)} %get-tuple-element.67), channel_id=1, source_target_pairs={{1,0},{2,1},{3,2},{4,3},{5,4},{6,5},{7,6},{8,7},{9,8},{10,9},{11,1... | collective-permute-start | bytes 2312 | tf_op jit(solution)/shard_map/ppermute | solution.py:20
  208.4 12.4 %copy-start.20 = (f32[1024]{0:T(1024)S(1)}, f32[1024]{0:T(1024)}, u32[]{:S(2)}) copy-start(f32[1024]{0:T(1024)} %param.21) | copy-start | bytes 12292
  208.4 12.4 %copy-start.21 = (f32[1024]{0:T(1024)S(1)}, f32[1024]{0:T(1024)}, u32[]{:S(2)}) copy-start(f32[1024]{0:T(1024)} %param.20) | copy-start | bytes 12292
  208.4 12.4 %copy-start.22 = (s32[1024]{0:T(1024)S(1)}, s32[1024]{0:T(1024)}, u32[]{:S(2)}) copy-start(s32[1024]{0:T(1024)} %param.19) | copy-start | bytes 12292
  232.8 3.8 %collective-permute-start.4 = (f32[4,4,256]{2,1,0:T(4,128)S(1)}, f32[4,4,256]{2,1,0:T(4,128)S(1)}, u32[]{:S(2)}, u32[]{:S(2)}) collective-permute-start(f32[4,4,256]{2,1,0:T(4,128)S(1)} %get-tuple-element.68), channel_id=1, source_target_pairs={{0,16},{16,0},{1,17},{17,1},{2,18},{18,2},{3,19},{19,3},{4,20},{20... | collective-permute-start | bytes 49160 | tf_op jit(solution)/shard_map/ppermute | solution.py:17
  234.7 3.7 %collective-permute-start.5 = (f32[4,4,256]{2,1,0:T(4,128)S(1)}, f32[4,4,256]{2,1,0:T(4,128)S(1)}, u32[]{:S(2)}, u32[]{:S(2)}) collective-permute-start(f32[4,4,256]{2,1,0:T(4,128)S(1)} %get-tuple-element.69), channel_id=1, source_target_pairs={{16,0},{0,16},{17,1},{1,17},{18,2},{2,18},{19,3},{3,19},{20,4},{4,... | collective-permute-start | bytes 49160 | tf_op jit(solution)/shard_map/ppermute | solution.py:20
  238.6 10.4 %collective-permute-start.6 = (f32[4,16,4]{2,1,0:T(8,128)S(1)}, f32[4,16,4]{2,1,0:T(8,128)S(1)}, u32[]{:S(2)}, u32[]{:S(2)}) collective-permute-start(f32[4,16,4]{2,1,0:T(8,128)S(1)} %get-tuple-element.64), channel_id=1, source_target_pairs={{0,1},{1,2},{2,3},{3,4},{4,5},{5,6},{6,7},{7,8},{8,9},{9,10},{10,1... | collective-permute-start | bytes 3080 | tf_op jit(solution)/shard_map/ppermute | solution.py:17
  238.6 10.4 %collective-permute-start.7 = (f32[4,16,4]{2,1,0:T(8,128)S(1)}, f32[4,16,4]{2,1,0:T(8,128)S(1)}, u32[]{:S(2)}, u32[]{:S(2)}) collective-permute-start(f32[4,16,4]{2,1,0:T(8,128)S(1)} %get-tuple-element.65), channel_id=1, source_target_pairs={{1,0},{2,1},{3,2},{4,3},{5,4},{6,5},{7,6},{8,7},{9,8},{10,9},{11,1... | collective-permute-start | bytes 3080 | tf_op jit(solution)/shard_map/ppermute | solution.py:20
  249.0 19.1 %copy-start.5 = (f32[4096,256]{1,0:T(8,128)S(1)}, f32[4096,256]{1,0:T(8,128)}, u32[]{:S(2)}) copy-start(f32[4096,256]{1,0:T(8,128)} %get-tuple-element.96) | copy-start | bytes 12582916
  268.1 4.9 %copy-start.9 = (f32[4096,256]{1,0:T(8,128)S(1)}, f32[4096,256]{1,0:T(8,128)}, u32[]{:S(2)}) copy-start(f32[4096,256]{1,0:T(8,128)} %get-tuple-element.98) | copy-start | bytes 12582916
  268.1 4.9 %copy-start.11 = (f32[4096,256]{1,0:T(8,128)S(1)}, f32[4096,256]{1,0:T(8,128)}, u32[]{:S(2)}) copy-start(f32[4096,256]{1,0:T(8,128)} %get-tuple-element.99) | copy-start | bytes 12582916
  273.0 4.1 %copy-start.13 = (f32[4096,256]{1,0:T(8,128)S(1)}, f32[4096,256]{1,0:T(8,128)}, u32[]{:S(2)}) copy-start(f32[4096,256]{1,0:T(8,128)} %get-tuple-element.100) | copy-start | bytes 12582916
  273.1 4.1 %copy-start.15 = (f32[4096,256]{1,0:T(8,128)S(1)}, f32[4096,256]{1,0:T(8,128)}, u32[]{:S(2)}) copy-start(f32[4096,256]{1,0:T(8,128)} %get-tuple-element.101) | copy-start | bytes 12582916
  277.2 4.1 %copy-start.1 = (f32[4096,256]{1,0:T(8,128)S(1)}, f32[4096,256]{1,0:T(8,128)}, u32[]{:S(2)}) copy-start(f32[4096,256]{1,0:T(8,128)} %get-tuple-element.106) | copy-start | bytes 12582916
  277.2 4.1 %copy-start.3 = (f32[4096,256]{1,0:T(8,128)S(1)}, f32[4096,256]{1,0:T(8,128)}, u32[]{:S(2)}) copy-start(f32[4096,256]{1,0:T(8,128)} %get-tuple-element.107) | copy-start | bytes 12582916
  299.7 7.0 %copy-start.7 = (f32[4096,256]{1,0:T(8,128)S(1)}, f32[4096,256]{1,0:T(8,128)}, u32[]{:S(2)}) copy-start(f32[4096,256]{1,0:T(8,128)} %get-tuple-element.97) | copy-start | bytes 12582916
  336.4 21.4 %copy-start.17 = (f32[10,16,256]{2,1,0:T(8,128)S(1)}, f32[10,16,256]{2,1,0:T(8,128)}, u32[]{:S(2)}) copy-start(f32[10,16,256]{2,1,0:T(8,128)} %param.13) | copy-start | bytes 491524
Sparse Core Ops, SparseCore 0:
  184.5 7.4 reduce-scatter.1
where the time goes:
time: 372 us; the launch traced here: 366 us
  other arithmetic  137 us (37%)
  matrix products  95.2 us (26%)
  local copies, waits for them, and re-layouts  43.3 us (12%)
  blocking collectives  28.1 us (8%)
  starting transfers between devices  26.5 us (7%)
  waiting for transfers between devices  20.1 us (5%)
  between operations  15.3 us (4%)
    dot_general x8, matrix products, spectral_filter(): jnp.dot(coeffs * weights[None, :], fourier_basis.T, precision=lax.Precisi...  56.9 us
    cos x3, other arithmetic, spectral_filter(): jnp.cos(radians)  53.6 us
    unnamed x6, other arithmetic  42.2 us
    dot_general x8, matrix products, spectral_filter(): jnp.dot(rows_data, fourier_basis, precision=lax.Precision.HIGHEST, prefer...  38.3 us
    gather x3, local copies, waits for them, and re-layouts, per_device(): values = states[moment][0].reshape(-1)[local_index]  18.5 us
    scatter-add x3, other arithmetic, per_device(): jnp.zeros((tile_rows * tile_cols,), jnp.float32).at[local_index]  17.9 us
    sin x1, other arithmetic, spectral_filter(): jnp.sin(radians)  17.6 us
    unnamed x68, local copies, waits for them, and re-layouts  14.9 us
  transfers between devices with their start and end apart: 11, of which 6 were waited for; matrix products, arithmetic and copies ran while one was open for 23% of the time, Pallas kernels for 0%

commit v1 on v0

--- a/solution.py
+++ b/solution.py
@@ -176,7 +176,12 @@
         lax.all_gather(half, "grp", axis=1, tiled=True),
         preferred_element_type=jnp.float32,
     )
-    filtered = lax.all_to_all(to_rows(weighted), "sp", split_axis=2, concat_axis=1, tiled=True)
+    filtered = jnp.concatenate(
+        lax.all_to_all(
+            jnp.stack(jnp.split(to_rows(weighted), lax.axis_size("sp"), axis=2)), "sp", 0, 0
+        ),
+        axis=1,
+    )
     grad_alpha = alpha + spread * filtered
     return (grad_alpha, grad_control)
 

time: 372 us -> 339 us (0.911)
  other arithmetic: 137 us -> 116 us
  local copies, waits for them, and re-layouts: 43.3 us -> 31.8 us
    unnamed x6 -> x5, other arithmetic: 42.2 us -> 22.6 us
    unnamed x68 -> x79, local copies, waits for them, and re-layouts: 14.9 us -> 7.67 us
  transfers between devices with their start and end apart: 11 -> 11, of which waited for: 6 -> 6; matrix products, arithmetic and copies ran while one was open for 23% -> 25% of each run, Pallas kernels for 0% -> 0%
where the time goes in v1:
time: 339 us; the launch traced here: 333 us
  other arithmetic  116 us (34%)
  matrix products  95.2 us (28%)
  local copies, waits for them, and re-layouts  31.8 us (9%)
  blocking collectives  28.1 us (8%)
  starting transfers between devices  26.5 us (8%)
  waiting for transfers between devices  20.1 us (6%)
  between operations  15.2 us (4%)
    dot_general x8, matrix products, spectral_filter(): jnp.dot(coeffs * weights[None, :], fourier_basis.T, precision=lax.Precisi...  56.9 us
    cos x3, other arithmetic, spectral_filter(): jnp.cos(radians)  53.6 us
    dot_general x8, matrix products, spectral_filter(): jnp.dot(rows_data, fourier_basis, precision=lax.Precision.HIGHEST, prefer...  38.3 us
    unnamed x5, other arithmetic  22.6 us
    gather x3, local copies, waits for them, and re-layouts, per_device(): values = states[moment][0].reshape(-1)[local_index]  18.5 us
    scatter-add x3, other arithmetic, per_device(): jnp.zeros((tile_rows * tile_cols,), jnp.float32).at[local_index]  17.9 us
    sin x1, other arithmetic, spectral_filter(): jnp.sin(radians)  17.6 us
    all_to_all x1, blocking collectives, to_rows(): lax.all_to_all(columns, 'sp', split_axis=1, concat_axis=2, tiled=True)  12.6 us
  transfers between devices with their start and end apart: 11, of which 6 were waited for; matrix products, arithmetic and copies ran while one was open for 25% of the time, Pallas kernels for 0%

profile of v1, /device:TPU:0, one launch (start us, length us, event | category | flops | bytes accessed | tf_op | source)
XLA Modules:
  0.0 333.0 jit_solution(13416457618077398377)
XLA Ops:
  7.2 1.7 copy.20
  8.9 7.4 %all-to-all-start = ((f32[10,16,256]{2,0,1:T(8,128)}), f32[10,16,256]{2,0,1:T(8,128)S(1)}, u32[]{:S(2)}, u32[]{:S(2)}) async-start(f32[10,16,256]{2,0,1:T(8,128)} %copy.20), calls=%async_computation | async-start | bytes 524288 | tf_op jit(solution)/shard_map/all_to_all | solution.py:130
  16.3 17.6 %fusion.37 = (f32[4096,256]{1,0:T(8,128)}, f32[4096,256]{1,0:T(8,128)}) fusion(), kind=kLoop, calls=%fused_computation.65 | loop fusion | flops 14680064 | bytes 8388608 | tf_op jit(solution)/shard_map/sin | solution.py:35
  34.0 17.9 %fusion.44 = (f32[4096,256]{1,0:T(8,128)}, f32[4096,256]{1,0:T(8,128)}) fusion(s32[256]{0:T(256)S(1)} %iota_add_fusion.2), kind=kLoop, calls=%fused_computation.72 | loop fusion | flops 14680064 | bytes 8389632 | tf_op jit(solution)/shard_map/cos | solution.py:35
  51.8 17.9 %fusion.42 = (f32[4096,256]{1,0:T(8,128)}, f32[4096,256]{1,0:T(8,128)}) fusion(s32[256]{0:T(256)S(1)} %iota_add_fusion.1), kind=kLoop, calls=%fused_computation.70 | loop fusion | flops 14680064 | bytes 8389632 | tf_op jit(solution)/shard_map/cos | solution.py:35
  69.7 17.8 %fusion.40 = (f32[4096,256]{1,0:T(8,128)}, f32[4096,256]{1,0:T(8,128)}) fusion(s32[256]{0:T(256)S(1)} %iota_add_fusion), kind=kLoop, calls=%fused_computation.68 | loop fusion | flops 14680064 | bytes 8389632 | tf_op jit(solution)/shard_map/cos | solution.py:35
  88.0 7.5 %fusion.45 = f32[512,10]{0,1:T(8,128)S(1)} fusion(f32[10,4096]{1,0:T(8,128)S(1)} %bitcast.234, f32[4096,256]{1,0:T(8,128)} %get-tuple-element.112, f32[4096,256]{1,0:T(8,128)} %get-tuple-element.113, f32[512]{0:T(512)S(1)} %get-tuple-element.108), kind=kOutput, calls=%fused_computation.73 | convolution fusion | flops 253760512 | bytes 8574976 | tf_op jit(solution)/shard_map/dot_general | solution.py:38
  95.5 7.0 %fusion.35 = f32[10,4096]{1,0:T(8,128)S(1)} fusion(f32[512,10]{0,1:T(8,128)S(1)} %fusion.45, f32[4096,256]{1,0:T(8,128)S(1)} %copy-done, f32[4096,256]{1,0:T(8,128)S(1)} %copy-done.2), kind=kOutput, calls=%fused_computation.63 | convolution fusion | flops 253755392 | bytes 8572928 | tf_op jit(solution)/shard_map/dot_general | solution.py:44
  102.5 4.5 %fusion.47 = f32[512,10]{0,1:T(8,128)S(1)} fusion(f32[10,4096]{1,0:T(8,128)S(1)} %bitcast.235, f32[4096,256]{1,0:T(8,128)S(1)} %copy-done.14, f32[4096,256]{1,0:T(8,128)S(1)} %copy-done.12, f32[512]{0:T(512)S(1)} %get-tuple-element.109), kind=kOutput, calls=%fused_computation.75 | convolution fusion | flops 253760512 | bytes 8574976 | tf_op jit(solution)/shard_map/dot_general | solution.py:38
  107.0 7.2 %convolution_add_fusion.5 = f32[10,4096]{1,0:T(8,128)S(1)} fusion(f32[10,4096]{1,0:T(8,128)S(1)} %fusion.35, f32[512,10]{0,1:T(8,128)S(1)} %fusion.47, f32[4096,256]{1,0:T(8,128)S(1)} %copy-done.14, f32[4096,256]{1,0:T(8,128)S(1)} %copy-done.12), kind=kOutput, calls=%fused_computation.28 | convolution fusion | flops 253796352 | bytes 8736768 | tf_op jit(solution)/shard_map/dot_general | solution.py:44
  114.2 4.5 %fusion.49 = f32[512,10]{0,1:T(8,128)S(1)} fusion(f32[10,4096]{1,0:T(8,128)S(1)} %bitcast.236, f32[4096,256]{1,0:T(8,128)S(1)} %copy-done.10, f32[4096,256]{1,0:T(8,128)S(1)} %copy-done.8, f32[512]{0:T(512)S(1)} %get-tuple-element.110), kind=kOutput, calls=%fused_computation.77 | convolution fusion | flops 253760512 | bytes 8574976 | tf_op jit(solution)/shard_map/dot_general | solution.py:38
  118.7 7.4 %convolution_add_fusion.4 = f32[10,4096]{1,0:T(8,128)S(1)} fusion(f32[10,4096]{1,0:T(8,128)S(1)} %convolution_add_fusion.5, f32[512,10]{0,1:T(8,128)S(1)} %fusion.49, f32[4096,256]{1,0:T(8,128)S(1)} %copy-done.10, f32[4096,256]{1,0:T(8,128)S(1)} %copy-done.8), kind=kOutput, calls=%fused_computation.27 | convolution fusion | flops 253796352 | bytes 8736768 | tf_op jit(solution)/shard_map/dot_general | solution.py:44
  126.2 4.5 %fusion.51 = f32[512,10]{0,1:T(8,128)S(1)} fusion(f32[10,4096]{1,0:T(8,128)S(1)} %bitcast.237, f32[4096,256]{1,0:T(8,128)S(1)} %copy-done.6, f32[4096,256]{1,0:T(8,128)S(1)} %copy-done.4, f32[512]{0:T(512)S(1)} %get-tuple-element.111), kind=kOutput, calls=%fused_computation.79 | convolution fusion | flops 253760512 | bytes 8574976 | tf_op jit(solution)/shard_map/dot_general | solution.py:38
  130.6 7.2 %fusion.2 = bf16[10,1,4096]{2,0,1:T(8,128)(2,1)S(1)} fusion(f32[10,4096]{1,0:T(8,128)S(1)} %convolution_add_fusion.4, f32[512,10]{0,1:T(8,128)S(1)} %fusion.51, f32[4096,256]{1,0:T(8,128)S(1)} %copy-done.6, f32[4096,256]{1,0:T(8,128)S(1)} %copy-done.4), kind=kOutput, calls=%fused_computation.30 | convolution fusion | flops 253837312 | bytes 8654848 | tf_op jit(solution)/shard_map/dot_general | solution.py:44
  137.8 2.8 copy.22
  141.2 22.5 %reduce.8 = bf16[4096,10]{1,0:T(8,128)(2,1)S(1)} reduce(bf16[4096,1,10]{2,1,0:T(2,128)(2,1)S(1)} %bitcast.223, bf16[]{:T(256)} %broadcast.394), dimensions={1}, to_apply=%bitcast.201.reduce_sub_computation | reduce | bytes 163842
  163.6 2.5 reshape.231
  166.1 6.0 %all-to-all-start.1 = ((bf16[16,2,1280]{2,1,0:T(2,128)(2,1)}), bf16[16,2,1280]{2,1,0:T(2,128)(2,1)S(1)}, u32[]{:S(2)}, u32[]{:S(2)}) async-start(bf16[16,2,1280]{2,1,0:T(2,128)(2,1)} %reshape.231), calls=%async_computation.1 | async-start | bytes 163840 | tf_op jit(solution)/shard_map/all_to_all | solution.py:133
  172.2 7.0 %all-to-all-done.1 = bf16[16,2,1280]{2,1,0:T(2,128)(2,1)S(1)} async-done(((bf16[16,2,1280]{2,1,0:T(2,128)(2,1)}), bf16[16,2,1280]{2,1,0:T(2,128)(2,1)S(1)}, u32[]{:S(2)}, u32[]{:S(2)}) %all-to-all-start.1) | async-done | bytes 81952 | tf_op jit(solution)/shard_map/all_to_all | solution.py:133
  179.2 2.2 reshape.232
  181.5 2.1 copy.23
  184.4 7.6 %reduce-scatter.2.cloned.1.call-done = f32[3,8,256]{2,1,0:T(8,128)} async-done(((f32[3,16,256]{2,1,0:T(8,128)}), f32[3,8,256]{2,1,0:T(8,128)}) %reduce-scatter.2.cloned.1.call-update) | async-done | bytes 24592 | tf_op jit(solution)/shard_map/reduce_scatter | solution.py:139
  192.0 0.7 multiply_add_fusion.1
  193.0 1.8 collective-permute-start.1
  194.8 1.7 collective-permute-done
  196.8 4.4 %collective-permute-start.3 = (f32[3,16,4]{2,1,0:T(8,128)S(1)}, f32[3,16,4]{2,1,0:T(8,128)S(1)}, u32[]{:S(2)}, u32[]{:S(2)}) collective-permute-start(f32[3,16,4]{2,1,0:T(8,128)S(1)} %get-tuple-element.73), channel_id=1, source_target_pairs={{1,0},{2,1},{3,2},{4,3},{5,4},{6,5},{7,6},{8,7},{9,8},{10,9},{11,1... | collective-permute-start | bytes 2312 | tf_op jit(solution)/shard_map/ppermute | solution.py:20
  201.2 6.1 %gather_fusion.2 = f32[1024]{0:T(1024)S(1)} fusion(f32[2048]{0:T(1024)S(1)} %bitcast.221, s32[1024]{0:T(1024)S(1)} %get-tuple-element.36), kind=kCustom, calls=%fused_computation.2 | custom fusion | bytes 12288 | tf_op jit(solution)/shard_map/gather | solution.py:149
  208.4 6.2 %gather_fusion = f32[1024]{0:T(1024)S(1)} fusion(f32[2048]{0:T(1024)S(1)} %bitcast.222, s32[1024]{0:T(1024)S(1)} %get-tuple-element.36), kind=kCustom, calls=%fused_computation | custom fusion | bytes 12288 | tf_op jit(solution)/shard_map/gather | solution.py:149
  214.6 6.2 %gather_fusion.1 = f32[1024]{0:T(1024)S(1)} fusion(f32[2048]{0:T(1024)S(1)} %bitcast.220, s32[1024]{0:T(1024)S(1)} %get-tuple-element.36), kind=kCustom, calls=%fused_computation.1 | custom fusion | bytes 12288 | tf_op jit(solution)/shard_map/gather | solution.py:149
  220.8 6.0 %scatter_custom_fusion = f32[2048]{0:T(1024)S(1)} fusion(s32[1024]{0:T(1024)S(1)} %get-tuple-element.37, f32[1024]{0:T(1024)S(1)} %get-tuple-element.96, f32[]{:T(128)} %constant.175.clone.1), kind=kCustom, calls=%fused_computation.258 | custom fusion | flops 1024 | bytes 8196 | tf_op jit(solution)/shard_map/scatter-add | solution.py:156
  226.8 6.0 %scatter_custom_fusion.1 = f32[2048]{0:T(1024)S(1)} fusion(s32[1024]{0:T(1024)S(1)} %get-tuple-element.37, f32[1024]{0:T(1024)S(1)} %get-tuple-element.97, f32[]{:T(128)} %constant.175.clone.1), kind=kCustom, calls=%fused_computation.256 | custom fusion | flops 1024 | bytes 8196 | tf_op jit(solution)/shard_map/scatter-add | solution.py:156
  232.8 2.0 collective-permute-start.4
  234.9 1.7 collective-permute-done.4
  236.6 1.9 collective-permute-done.5
  238.6 4.4 %collective-permute-start.7 = (f32[4,16,4]{2,1,0:T(8,128)S(1)}, f32[4,16,4]{2,1,0:T(8,128)S(1)}, u32[]{:S(2)}, u32[]{:S(2)}) collective-permute-start(f32[4,16,4]{2,1,0:T(8,128)S(1)} %get-tuple-element.71), channel_id=1, source_target_pairs={{1,0},{2,1},{3,2},{4,3},{5,4},{6,5},{7,6},{8,7},{9,8},{10,9},{11,1... | collective-permute-start | bytes 3080 | tf_op jit(solution)/shard_map/ppermute | solution.py:20
  243.1 6.0 %scatter_custom_fusion.2 = f32[2048]{0:T(1024)S(1)} fusion(s32[1024]{0:T(1024)S(1)} %get-tuple-element.37, f32[1024]{0:T(1024)S(1)} %get-tuple-element.32, f32[]{:T(128)} %constant.175.clone.1), kind=kCustom, calls=%fused_computation.254 | custom fusion | flops 1024 | bytes 8196 | tf_op jit(solution)/shard_map/scatter-add | solution.py:156
  250.7 4.4 %all_gather.3 = bf16[3,16,256]{2,1,0:T(8,128)(2,1)S(1)} all-gather(bf16[3,8,256]{2,1,0:T(8,128)(2,1)S(1)} %get-tuple-element.77), channel_id=1, replica_groups=mesh['grp'=2,'sp'=16] {'grp'}, dimensions={1}, use_global_device_ids=true | all-gather | bytes 36864 | tf_op jit(solution)/shard_map/all_gather | solution.py:176
  255.2 12.6 %all_to_all.35 = f32[10,16,256]{2,0,1:T(8,128)S(1)} all-to-all(f32[10,16,256]{2,0,1:T(8,128)S(1)} %bitcast.231), channel_id=1, replica_groups=mesh['grp'=2,'sp'=16] {'sp'}, dimensions={1} | all-to-all | bytes 327680 | tf_op jit(solution)/shard_map/all_to_all | solution.py:130
  268.2 4.9 %fusion.52 = f32[10,512]{1,0:T(8,128)S(1)} fusion(f32[10,4096]{1,0:T(8,128)S(1)} %bitcast.225, f32[4096,256]{1,0:T(8,128)} %get-tuple-element.103, f32[4096,256]{1,0:T(8,128)S(1)} %copy-done.5, f32[512]{0:T(512)S(1)} %get-tuple-element.111), kind=kOutput, calls=%fused_computation.80 | convolution fusion | flops 253760512 | bytes 8574976 | tf_op jit(solution)/shard_map/dot_general | solution.py:38
  273.1 4.1 %fusion.50 = f32[10,512]{1,0:T(8,128)S(1)} fusion(f32[10,4096]{1,0:T(8,128)S(1)} %bitcast.226, f32[4096,256]{1,0:T(8,128)S(1)} %copy-done.11, f32[4096,256]{1,0:T(8,128)S(1)} %copy-done.9, f32[512]{0:T(512)S(1)} %get-tuple-element.110), kind=kOutput, calls=%fused_computation.78 | convolution fusion | flops 253760512 | bytes 8574976 | tf_op jit(solution)/shard_map/dot_general | solution.py:38
  277.2 4.1 %fusion.48 = f32[10,512]{1,0:T(8,128)S(1)} fusion(f32[10,4096]{1,0:T(8,128)S(1)} %bitcast.227, f32[4096,256]{1,0:T(8,128)S(1)} %copy-done.15, f32[4096,256]{1,0:T(8,128)S(1)} %copy-done.13, f32[512]{0:T(512)S(1)} %get-tuple-element.109), kind=kOutput, calls=%fused_computation.76 | convolution fusion | flops 253760512 | bytes 8574976 | tf_op jit(solution)/shard_map/dot_general | solution.py:38
  281.3 4.3 %fusion.46 = f32[10,512]{1,0:T(8,128)S(1)} fusion(f32[10,4096]{1,0:T(8,128)S(1)} %bitcast.228, f32[4096,256]{1,0:T(8,128)S(1)} %copy-done.1, f32[4096,256]{1,0:T(8,128)S(1)} %copy-done.3, f32[512]{0:T(512)S(1)} %get-tuple-element.108), kind=kOutput, calls=%fused_computation.74 | convolution fusion | flops 253760512 | bytes 8574976 | tf_op jit(solution)/shard_map/dot_general | solution.py:38
  285.5 7.0 %fusion.33 = f32[10,4096]{1,0:T(8,128)S(1)} fusion(f32[10,512]{1,0:T(8,128)S(1)} %fusion.46, f32[4096,256]{1,0:T(8,128)S(1)} %copy-done.1, f32[4096,256]{1,0:T(8,128)S(1)} %copy-done.3), kind=kOutput, calls=%fused_computation.61 | convolution fusion | flops 253755392 | bytes 8572928 | tf_op jit(solution)/shard_map/dot_general | solution.py:44
  292.5 7.2 %convolution_add_fusion.2 = f32[10,4096]{1,0:T(8,128)S(1)} fusion(f32[10,4096]{1,0:T(8,128)S(1)} %fusion.33, f32[10,512]{1,0:T(8,128)S(1)} %fusion.48, f32[4096,256]{1,0:T(8,128)S(1)} %copy-done.15, f32[4096,256]{1,0:T(8,128)S(1)} %copy-done.13), kind=kOutput, calls=%fused_computation.25 | convolution fusion | flops 253796352 | bytes 8736768 | tf_op jit(solution)/shard_map/dot_general | solution.py:44
  299.7 7.0 %convolution_add_fusion.1 = f32[10,4096]{1,0:T(8,128)S(1)} fusion(f32[10,4096]{1,0:T(8,128)S(1)} %convolution_add_fusion.2, f32[10,512]{1,0:T(8,128)S(1)} %fusion.50, f32[4096,256]{1,0:T(8,128)S(1)} %copy-done.11, f32[4096,256]{1,0:T(8,128)S(1)} %copy-done.9), kind=kOutput, calls=%fused_computation.24 | convolution fusion | flops 253796352 | bytes 8736768 | tf_op jit(solution)/shard_map/dot_general | solution.py:44
  306.8 7.0 %fusion = f32[10,1,4096]{2,0,1:T(8,128)S(1)} fusion(f32[10,4096]{1,0:T(8,128)S(1)} %convolution_add_fusion.1, f32[10,512]{1,0:T(8,128)S(1)} %fusion.52, f32[4096,256]{1,0:T(8,128)S(1)} %copy-done.7, f32[4096,256]{1,0:T(8,128)S(1)} %copy-done.5), kind=kOutput, calls=%fused_computation.23 | convolution fusion | flops 253796352 | bytes 8736768 | tf_op jit(solution)/shard_map/dot_general | solution.py:44
  314.1 11.1 %all_to_all.36 = f32[16,10,1,256]{3,2,1,0:T(1,128)S(1)} all-to-all(f32[16,10,1,256]{3,2,1,0:T(1,128)S(1)} %copy.25), channel_id=1, replica_groups=mesh['grp'=2,'sp'=16] {'sp'}, dimensions={0} | all-to-all | bytes 327680 | tf_op jit(solution)/shard_map/all_to_all | solution.py:180
  325.3 0.7 bitcast_add_fusion
  (152 shorter events, 5.8 us)
Async XLA Ops:
  8.9 78.7 %all-to-all-start = ((f32[10,16,256]{2,0,1:T(8,128)}), f32[10,16,256]{2,0,1:T(8,128)S(1)}, u32[]{:S(2)}, u32[]{:S(2)}) async-start(f32[10,16,256]{2,0,1:T(8,128)} %copy.20), calls=%async_computation | async-start | bytes 524288 | tf_op jit(solution)/shard_map/all_to_all | solution.py:130
  16.3 17.7 %copy-start.23 = (f32[1024]{0:T(1024)S(1)}, f32[1024]{0:T(1024)}, u32[]{:S(2)}) copy-start(f32[1024]{0:T(1024)} %param.17) | copy-start | bytes 12292
  69.7 17.9 %copy-start.24 = (s32[1024]{0:T(1024)S(1)}, s32[1024]{0:T(1024)}, u32[]{:S(2)}) copy-start(s32[1024]{0:T(1024)} %param.18) | copy-start | bytes 12292
  87.9 7.5 %copy-start = (f32[4096,256]{1,0:T(8,128)S(1)}, f32[4096,256]{1,0:T(8,128)}, u32[]{:S(2)}) copy-start(f32[4096,256]{1,0:T(8,128)} %get-tuple-element.112) | copy-start | bytes 12582916
  87.9 7.5 %copy-start.2 = (f32[4096,256]{1,0:T(8,128)S(1)}, f32[4096,256]{1,0:T(8,128)}, u32[]{:S(2)}) copy-start(f32[4096,256]{1,0:T(8,128)} %get-tuple-element.113) | copy-start | bytes 12582916
  95.5 7.0 %copy-start.12 = (f32[4096,256]{1,0:T(8,128)S(1)}, f32[4096,256]{1,0:T(8,128)}, u32[]{:S(2)}) copy-start(f32[4096,256]{1,0:T(8,128)} %get-tuple-element.106) | copy-start | bytes 12582916
  95.5 7.0 %copy-start.14 = (f32[4096,256]{1,0:T(8,128)S(1)}, f32[4096,256]{1,0:T(8,128)}, u32[]{:S(2)}) copy-start(f32[4096,256]{1,0:T(8,128)} %get-tuple-element.107) | copy-start | bytes 12582916
  107.0 7.2 %copy-start.8 = (f32[4096,256]{1,0:T(8,128)S(1)}, f32[4096,256]{1,0:T(8,128)}, u32[]{:S(2)}) copy-start(f32[4096,256]{1,0:T(8,128)} %get-tuple-element.104) | copy-start | bytes 12582916
  107.0 7.2 %copy-start.10 = (f32[4096,256]{1,0:T(8,128)S(1)}, f32[4096,256]{1,0:T(8,128)}, u32[]{:S(2)}) copy-start(f32[4096,256]{1,0:T(8,128)} %get-tuple-element.105) | copy-start | bytes 12582916
  118.7 7.4 %copy-start.4 = (f32[4096,256]{1,0:T(8,128)S(1)}, f32[4096,256]{1,0:T(8,128)}, u32[]{:S(2)}) copy-start(f32[4096,256]{1,0:T(8,128)} %get-tuple-element.102) | copy-start | bytes 12582916
  118.7 7.4 %copy-start.6 = (f32[4096,256]{1,0:T(8,128)S(1)}, f32[4096,256]{1,0:T(8,128)}, u32[]{:S(2)}) copy-start(f32[4096,256]{1,0:T(8,128)} %get-tuple-element.103) | copy-start | bytes 12582916
  141.1 42.5 %copy-start.16 = (bf16[10,3,16,256]{3,2,1,0:T(8,128)(2,1)S(1)}, bf16[10,3,16,256]{3,2,1,0:T(8,128)(2,1)}, u32[]{:S(2)}) copy-start(bf16[10,3,16,256]{3,2,1,0:T(8,128)(2,1)} %param.14) | copy-start | bytes 737284
  141.2 50.8 %copy-start.18 = (f32[3,8,256]{2,1,0:T(8,128)S(1)}, f32[3,8,256]{2,1,0:T(8,128)}, u32[]{:S(2)}) copy-start(f32[3,8,256]{2,1,0:T(8,128)} %param.16) | copy-start | bytes 73732
  141.2 50.8 %copy-start.19 = (f32[3,8,256]{2,1,0:T(8,128)S(1)}, f32[3,8,256]{2,1,0:T(8,128)}, u32[]{:S(2)}) copy-start(f32[3,8,256]{2,1,0:T(8,128)} %param.15) | copy-start | bytes 73732
  166.1 13.1 %all-to-all-start.1 = ((bf16[16,2,1280]{2,1,0:T(2,128)(2,1)}), bf16[16,2,1280]{2,1,0:T(2,128)(2,1)S(1)}, u32[]{:S(2)}, u32[]{:S(2)}) async-start(bf16[16,2,1280]{2,1,0:T(2,128)(2,1)} %reshape.231), calls=%async_computation.1 | async-start | bytes 163840 | tf_op jit(solution)/shard_map/all_to_all | solution.py:133
  172.1 19.9 %reduce-scatter.2.cloned.1.call-start = ((), (), s32[]{:S(2)}) async-start(), calls=%async_computation.5 | async-start | bytes 73728 | tf_op jit(solution)/shard_map/reduce_scatter | solution.py:139
  192.7 3.8 %collective-permute-start = (f32[3,4,256]{2,1,0:T(4,128)S(1)}, f32[3,4,256]{2,1,0:T(4,128)S(1)}, u32[]{:S(2)}, u32[]{:S(2)}) collective-permute-start(f32[3,4,256]{2,1,0:T(4,128)S(1)} %get-tuple-element.94), channel_id=1, source_target_pairs={{0,16},{16,0},{1,17},{17,1},{2,18},{18,2},{3,19},{19,3},{4,20},{20... | collective-permute-start | bytes 36872 | tf_op jit(solution)/shard_map/ppermute | solution.py:17
  193.0 3.7 %collective-permute-start.1 = (f32[3,4,256]{2,1,0:T(4,128)S(1)}, f32[3,4,256]{2,1,0:T(4,128)S(1)}, u32[]{:S(2)}, u32[]{:S(2)}) collective-permute-start(f32[3,4,256]{2,1,0:T(4,128)S(1)} %get-tuple-element.95), channel_id=1, source_target_pairs={{16,0},{0,16},{17,1},{1,17},{18,2},{2,18},{19,3},{3,19},{20,4},{4,... | collective-permute-start | bytes 36872 | tf_op jit(solution)/shard_map/ppermute | solution.py:20
  196.8 10.6 %collective-permute-start.2 = (f32[3,16,4]{2,1,0:T(8,128)S(1)}, f32[3,16,4]{2,1,0:T(8,128)S(1)}, u32[]{:S(2)}, u32[]{:S(2)}) collective-permute-start(f32[3,16,4]{2,1,0:T(8,128)S(1)} %get-tuple-element.72), channel_id=1, source_target_pairs={{0,1},{1,2},{2,3},{3,4},{4,5},{5,6},{6,7},{7,8},{8,9},{9,10},{10,1... | collective-permute-start | bytes 2312 | tf_op jit(solution)/shard_map/ppermute | solution.py:17
  196.8 10.6 %collective-permute-start.3 = (f32[3,16,4]{2,1,0:T(8,128)S(1)}, f32[3,16,4]{2,1,0:T(8,128)S(1)}, u32[]{:S(2)}, u32[]{:S(2)}) collective-permute-start(f32[3,16,4]{2,1,0:T(8,128)S(1)} %get-tuple-element.73), channel_id=1, source_target_pairs={{1,0},{2,1},{3,2},{4,3},{5,4},{6,5},{7,6},{8,7},{9,8},{10,9},{11,1... | collective-permute-start | bytes 2312 | tf_op jit(solution)/shard_map/ppermute | solution.py:20
  208.4 12.4 %copy-start.20 = (f32[1024]{0:T(1024)S(1)}, f32[1024]{0:T(1024)}, u32[]{:S(2)}) copy-start(f32[1024]{0:T(1024)} %param.21) | copy-start | bytes 12292
  208.4 12.4 %copy-start.21 = (f32[1024]{0:T(1024)S(1)}, f32[1024]{0:T(1024)}, u32[]{:S(2)}) copy-start(f32[1024]{0:T(1024)} %param.20) | copy-start | bytes 12292
  208.4 12.4 %copy-start.22 = (s32[1024]{0:T(1024)S(1)}, s32[1024]{0:T(1024)}, u32[]{:S(2)}) copy-start(s32[1024]{0:T(1024)} %param.19) | copy-start | bytes 12292
  232.8 3.8 %collective-permute-start.4 = (f32[4,4,256]{2,1,0:T(4,128)S(1)}, f32[4,4,256]{2,1,0:T(4,128)S(1)}, u32[]{:S(2)}, u32[]{:S(2)}) collective-permute-start(f32[4,4,256]{2,1,0:T(4,128)S(1)} %get-tuple-element.74), channel_id=1, source_target_pairs={{0,16},{16,0},{1,17},{17,1},{2,18},{18,2},{3,19},{19,3},{4,20},{20... | collective-permute-start | bytes 49160 | tf_op jit(solution)/shard_map/ppermute | solution.py:17
  234.8 3.7 %collective-permute-start.5 = (f32[4,4,256]{2,1,0:T(4,128)S(1)}, f32[4,4,256]{2,1,0:T(4,128)S(1)}, u32[]{:S(2)}, u32[]{:S(2)}) collective-permute-start(f32[4,4,256]{2,1,0:T(4,128)S(1)} %get-tuple-element.75), channel_id=1, source_target_pairs={{16,0},{0,16},{17,1},{1,17},{18,2},{2,18},{19,3},{3,19},{20,4},{4,... | collective-permute-start | bytes 49160 | tf_op jit(solution)/shard_map/ppermute | solution.py:20
  238.6 10.4 %collective-permute-start.6 = (f32[4,16,4]{2,1,0:T(8,128)S(1)}, f32[4,16,4]{2,1,0:T(8,128)S(1)}, u32[]{:S(2)}, u32[]{:S(2)}) collective-permute-start(f32[4,16,4]{2,1,0:T(8,128)S(1)} %get-tuple-element.70), channel_id=1, source_target_pairs={{0,1},{1,2},{2,3},{3,4},{4,5},{5,6},{6,7},{7,8},{8,9},{9,10},{10,1... | collective-permute-start | bytes 3080 | tf_op jit(solution)/shard_map/ppermute | solution.py:17
  238.6 10.4 %collective-permute-start.7 = (f32[4,16,4]{2,1,0:T(8,128)S(1)}, f32[4,16,4]{2,1,0:T(8,128)S(1)}, u32[]{:S(2)}, u32[]{:S(2)}) collective-permute-start(f32[4,16,4]{2,1,0:T(8,128)S(1)} %get-tuple-element.71), channel_id=1, source_target_pairs={{1,0},{2,1},{3,2},{4,3},{5,4},{6,5},{7,6},{8,7},{9,8},{10,9},{11,1... | collective-permute-start | bytes 3080 | tf_op jit(solution)/shard_map/ppermute | solution.py:20
  249.0 19.1 %copy-start.5 = (f32[4096,256]{1,0:T(8,128)S(1)}, f32[4096,256]{1,0:T(8,128)}, u32[]{:S(2)}) copy-start(f32[4096,256]{1,0:T(8,128)} %get-tuple-element.102) | copy-start | bytes 12582916
  268.1 4.9 %copy-start.9 = (f32[4096,256]{1,0:T(8,128)S(1)}, f32[4096,256]{1,0:T(8,128)}, u32[]{:S(2)}) copy-start(f32[4096,256]{1,0:T(8,128)} %get-tuple-element.104) | copy-start | bytes 12582916
  268.1 4.9 %copy-start.11 = (f32[4096,256]{1,0:T(8,128)S(1)}, f32[4096,256]{1,0:T(8,128)}, u32[]{:S(2)}) copy-start(f32[4096,256]{1,0:T(8,128)} %get-tuple-element.105) | copy-start | bytes 12582916
  273.1 4.1 %copy-start.13 = (f32[4096,256]{1,0:T(8,128)S(1)}, f32[4096,256]{1,0:T(8,128)}, u32[]{:S(2)}) copy-start(f32[4096,256]{1,0:T(8,128)} %get-tuple-element.106) | copy-start | bytes 12582916
  273.1 4.1 %copy-start.15 = (f32[4096,256]{1,0:T(8,128)S(1)}, f32[4096,256]{1,0:T(8,128)}, u32[]{:S(2)}) copy-start(f32[4096,256]{1,0:T(8,128)} %get-tuple-element.107) | copy-start | bytes 12582916
  277.2 4.1 %copy-start.1 = (f32[4096,256]{1,0:T(8,128)S(1)}, f32[4096,256]{1,0:T(8,128)}, u32[]{:S(2)}) copy-start(f32[4096,256]{1,0:T(8,128)} %get-tuple-element.112) | copy-start | bytes 12582916
  277.2 4.1 %copy-start.3 = (f32[4096,256]{1,0:T(8,128)S(1)}, f32[4096,256]{1,0:T(8,128)}, u32[]{:S(2)}) copy-start(f32[4096,256]{1,0:T(8,128)} %get-tuple-element.113) | copy-start | bytes 12582916
  299.7 7.0 %copy-start.7 = (f32[4096,256]{1,0:T(8,128)S(1)}, f32[4096,256]{1,0:T(8,128)}, u32[]{:S(2)}) copy-start(f32[4096,256]{1,0:T(8,128)} %get-tuple-element.103) | copy-start | bytes 12582916
  306.8 18.5 %copy-start.17 = (f32[10,16,256]{2,1,0:T(8,128)S(1)}, f32[10,16,256]{2,1,0:T(8,128)}, u32[]{:S(2)}) copy-start(f32[10,16,256]{2,1,0:T(8,128)} %param.13) | copy-start | bytes 491524
Sparse Core Ops, SparseCore 0:
  184.5 7.4 reduce-scatter.1
